TPU v7x, 32 devices: a whole 2x2x4 slice. The times are simulated.
32 devices in a mesh: groups: 2 (over y), rowt: 4 (over z), colt: 2 (over x), site: 2 (over core).
Axes of the slice: x: 2, y: 2, z: 4, core: 2. Of those that a mesh axis runs over, the one named last changes fastest.
Arguments:
- seed_green: bfloat16 [8, 2, 768, 768], P(('groups', 'rowt'), 'colt', None, 'site'), parts along dimension 0, may hold values from -6 to 6
- field_spins: int32 [4, 8, 768], P(None, ('groups', 'rowt')), parts along dimension 1, may hold values from 0 to 1
- hop_matrix: float32 [768, 768], replicated, may hold values from -0.21875 to 0.21875
- vertex: bfloat16 [768, 768], replicated, may hold values from -0.21875 to 0.21875
Outputs:
- measured: bfloat16 [8, 2, 768, 768], P(('groups', 'rowt'), 'colt', None, 'site'), parts along dimension 0
There are 2 independent parts, one for each index of `groups`. A program takes and returns all parts, laid end to end along the dimension named above; an argument that names none is the same for every part. Nothing has to cross between parts.
All inputs are finite; a program needn't handle non-finite values.
Results may differ from a plain program's by a relative error of at most 0.0051.
Values may be sent and summed in bfloat16 or wider, within the bound.
No kernel may reach another device: no remote copies, remote signals or barrier semaphores. Data moves between devices by JAX's collectives and lax.ppermute only.
A program may use at most 64 MiB of HBM per device.

v0:
```python
import functools

import jax
import jax.numpy as jnp
from jax import lax
from jax.experimental import pallas as pl
from jax.experimental.pallas import tpu as pltpu
from jax.sharding import PartitionSpec as P


coupling = 0.45
keep_share = 0.8
hop_share = 0.3
LANES = 128
PIECES = 4


VMEM = pl.BlockSpec(memory_space=pltpu.VMEM)
HBM = pl.BlockSpec(memory_space=pltpu.HBM)


def limit(mebibytes):
    return pltpu.CompilerParams(vmem_limit_bytes=mebibytes << 20)


def in_hbm(array):
    return pltpu.with_memory_space_constraint(array, pltpu.HBM)


def split_halves(value):
    high = value.astype(jnp.bfloat16)
    low = (value - high.astype(jnp.float32)).astype(jnp.bfloat16)
    return high, low


def site_spans(width):
    site = lax.axis_index("site")
    places = (site, lax.axis_size("site") - 1 - site)
    return [pl.ds(pl.multiple_of(place * width, LANES), width) for place in places]


def cut_kernel(seed_ref, piece, sems):
    width = seed_ref.shape[1]
    copies = []
    for half, source in enumerate(reversed(site_spans(width))):
        copy = pltpu.make_async_copy(
            seed_ref.at[source, pl.ds(0, piece.shape[1])],
            piece.at[pl.ds(half * width, width)],
            sems.at[half],
        )
        copy.start()
        copies.append(copy)
    for copy in copies:
        copy.wait()


def hold_kernel(spins_ref, seed_ref, lines_out, piece_out):
    lines = [spins_ref[step] for step in range(lines_out.shape[0])]
    lines_out[...] = jnp.concatenate(lines, axis=0).astype(jnp.float32).astype(jnp.bfloat16)
    width = seed_ref.shape[1]
    for half, source in enumerate(reversed(site_spans(width))):
        span = slice(half * width, (half + 1) * width)
        piece_out[span, :] = seed_ref[source, width - piece_out.shape[1] :]


def prepare_kernel(hop_ref, *refs):
    pieces = refs[:-4]
    hop_out, high_t, low_t, turned_out = refs[-4:]
    width, _ = turned_out.shape
    start = 0
    for piece in pieces:
        lines = slice(start, start + piece.shape[1])
        turned_out[lines, :width] = piece[width:, :].T
        turned_out[lines, width:] = piece[:width, :].T
        start += piece.shape[1]
    site = lax.axis_index("site")
    places = (site, lax.axis_size("site") - 1 - site)
    for half, place in enumerate(places):
        for start in range(0, width, LANES):
            rows = pl.ds(pl.multiple_of(place * width + start, LANES), LANES)
            strip = jnp.concatenate([hop_ref[rows, span] for span in site_spans(width)], axis=1)
            high, low = split_halves(hop_share * strip)
            spot = slice(half * width + start, half * width + start + LANES)
            hop_out[spot, :] = high
            high_t[:, spot] = high.T
            low_t[:, spot] = low.T


def hop_turned(narrow, high_t, low_t):
    hopped = jnp.dot(narrow, high_t[...], preferred_element_type=jnp.float32)
    if low_t is not None:
        hopped += jnp.dot(narrow, low_t[...], preferred_element_type=jnp.float32)
    return hopped


def lift_kernel(seed_t, high_t, low_t, _, image_out):
    narrow = seed_t[...]
    hopped = hop_turned(narrow, high_t, low_t)
    image_out[...] = keep_share * narrow.astype(jnp.float32) + hopped


def join_kernel(held_ref, came_ref, out_ref):
    out_ref[...] = jnp.concatenate([held_ref[...], came_ref[...]], axis=0)


def early_kernel(row_count, doubled, image_ref, high_t, low_t, *refs):
    *line_refs, turned_out, image_out, scale_out, column_out = refs
    wraps = scale_out.shape[0]
    row_index = lax.axis_index("rowt")
    lines = jnp.concatenate([ref[...].astype(jnp.float32) for ref in line_refs], axis=0)
    places = lax.broadcasted_iota(jnp.int32, lines.shape, 0)
    half = lines.shape[1] // 2
    other = jnp.concatenate([lines[:, half:], lines[:, :half]], axis=1)
    lines = jnp.where(lax.axis_index("site") == 0, lines, other)
    scales = []
    for step in range(wraps):
        target = (row_index + step + 1) % row_count
        if doubled:
            pick = (row_index ^ target) * wraps + step
            spins = jnp.sum(jnp.where(places == pick, lines, 0.0), axis=0, keepdims=True)
        else:
            spins = lines[step : step + 1]
        sign = jnp.where(target == 0, -1.0, 1.0)
        scales.append(sign * jnp.exp(coupling * (2.0 * spins - 1.0)))
    turned = scales[0] * image_ref[...]
    narrow = turned.astype(jnp.bfloat16)
    turned_out[0] = narrow
    image_out[...] = keep_share * turned + hop_turned(narrow, high_t, low_t)
    scale = jnp.concatenate(scales, axis=0)
    scale_out[...] = scale
    columns = scale.T
    for step in range(wraps):
        column_out[step] = jnp.broadcast_to(columns[:, step : step + 1], column_out.shape[1:])


def own_kernel(first, image_ref, high_t, low_t, scale_ref, turned_out, *rest):
    steps, wraps = turned_out.shape[0], scale_ref.shape[0]
    image = image_ref[...]
    for step in range(first, first + steps):
        turned = scale_ref[step : step + 1, :] * image
        narrow = turned.astype(jnp.bfloat16)
        turned_out[step - first] = narrow
        if step < wraps - 1:
            low = low_t if step < wraps - 2 else None
            image = keep_share * turned + hop_turned(narrow, high_t, low)
    if rest:
        rest[0][...] = image


def spread(columns, pieces):
    size = columns.shape[0] // pieces
    starts = range(0, columns.shape[0], size)
    return [columns[start : start + size].astype(jnp.float32) for start in starts]


def advance(step, halves, hop_ref, scale_ref, level, narrow):
    size, copies = level[0].shape[0], level[0].shape[1] // LANES
    source = jnp.concatenate(narrow, axis=0)
    new, fresh = [], []
    each = len(level) // 2
    for half in range(halves):
        for number in range(half * each, half * each + each):
            span = slice(number * size, (number + 1) * size)
            hopped = jnp.dot(hop_ref[span, :], source, preferred_element_type=jnp.float32)
            scale = jnp.concatenate([scale_ref[step, span, :]] * copies, axis=1)
            moved = scale * (keep_share * level[number] + hopped)
            new.append(moved)
            fresh.append(moved.astype(jnp.bfloat16))
        yield jnp.concatenate(fresh[half * each : half * each + each], axis=0)
    level[: len(new)] = new
    if halves == 2:
        narrow[:] = fresh


def chain_kernel(arrived, hop_ref, scale_ref, keep_out, send_out):
    level = spread(arrived[...], PIECES)
    narrow = [block.astype(jnp.bfloat16) for block in level]
    for step in range(keep_out.shape[0]):
        rounded = advance(step, 2, hop_ref, scale_ref, level, narrow)
        for value, out in zip(rounded, (keep_out, send_out)):
            out[step] = value


def multiply(met, own):
    return (met * own).astype(jnp.float32)


def own_levels(turned_refs, spans):
    for turned_ref in turned_refs:
        for step in range(turned_ref.shape[0]):
            parts = [turned_ref[step, :, span] for span in spans]
            yield parts[0] if len(parts) == 1 else jnp.concatenate(parts, axis=1)


def columns_at(offset, part, width):
    site = lax.axis_index("site")
    places = (lax.axis_size("site") - 1 - site, site)
    held = [slice(width + offset, width + offset + part), slice(offset, offset + part)]
    return held, [pl.ds(pl.multiple_of(p * width + offset, LANES), part) for p in places]


def against(corner, product):
    return lax.dot_general(
        corner, product, (((1,), (1,)), ((), ())), preferred_element_type=jnp.float32
    )


def sum_part(offset, which, met_ref, vertex_ref, turned_refs):
    _, width, part = met_ref.shape
    held, spots = columns_at(offset, part, width)
    pairs = None
    for step, own in enumerate(own_levels(turned_refs, [held[which]])):
        product = multiply(met_ref[step], own)
        pairs = product if pairs is None else pairs + product
    corner = vertex_ref[:, spots[which]]
    high, low = split_halves(pairs)
    return against(corner, high) + against(corner, low)


def add_kernel(offset, which, met_ref, vertex_ref, *refs):
    *turned_refs, out_ref = refs
    total = turned_refs.pop(0)[...] if which else 0.0
    out_ref[...] = total + sum_part(offset, which, met_ref, vertex_ref, turned_refs)


def fold_kernel(hop_ref, scale_ref, fold_out):
    width, wraps = fold_out.shape[0], scale_ref.shape[0]
    left = hop_ref[:width, :].astype(jnp.float32) * scale_ref[wraps - 2 : wraps - 1, :]
    right = jnp.dot(
        left.astype(jnp.bfloat16), hop_ref[...], preferred_element_type=jnp.float32
    )
    fold_out[...] = (keep_share * left + right).astype(jnp.bfloat16)


def finish_kernel(offset, *refs):
    ours, theirs, hop_ref, fold_ref, scale_ref, vertex_ref, total_ref, *turned_refs = refs[:-3]
    out_ref, result, sems = refs[-3:]
    wraps, (sites, width) = scale_ref.shape[0], total_ref.shape
    spans = [slice(0, width), slice(width, 2 * width)]
    held, spots = columns_at(offset, ours.shape[1], width)
    other = jnp.concatenate([theirs[span, :] for span in reversed(spans)], axis=0)
    level = spread(jnp.concatenate([ours[...], other], axis=1), PIECES)
    narrow = [block.astype(jnp.bfloat16) for block in level]
    pairs = None
    for step, own in enumerate(own_levels(turned_refs, held)):
        if step < wraps - 2:
            met, *_ = advance(step, 2, hop_ref, scale_ref, level, narrow)
        else:
            weights = hop_ref if step == wraps - 2 else fold_ref
            met, *_ = advance(step, 1, weights, scale_ref, level, narrow)
        product = multiply(met, own)
        pairs = product if pairs is None else pairs + product
    summed = pairs.astype(jnp.bfloat16)
    edges = [0, sites // 3, 2 * sites // 3, sites]
    copies = []
    for block, (begin, end) in enumerate(zip(edges, edges[1:])):
        span = slice(begin, end)
        corner = jnp.concatenate([vertex_ref[span, spot] for spot in spots], axis=1)
        total = total_ref[span, :] + against(corner, summed)
        result[span, :] = (total / wraps).astype(result.dtype)
        copy = pltpu.make_async_copy(
            result.at[pl.ds(begin, end - begin)],
            out_ref.at[pl.ds(begin, end - begin)],
            sems.at[block],
        )
        copy.start()
        copies.append(copy)
    for copy in copies:
        copy.wait()


def cut(seed, columns):
    return pl.pallas_call(
        cut_kernel,
        out_shape=jax.ShapeDtypeStruct((seed.shape[0], columns), jnp.bfloat16),
        in_specs=[HBM],
        out_specs=VMEM,
        scratch_shapes=[pltpu.SemaphoreType.DMA((2,))],
        compiler_params=limit(8),
        cost_estimate=pl.CostEstimate(flops=1 << 30, bytes_accessed=1 << 20, transcendentals=0),
        name="cut",
    )(in_hbm(seed))


def hold(spins, seed, columns):
    return pl.pallas_call(
        hold_kernel,
        out_shape=[
            jax.ShapeDtypeStruct((spins.shape[0], spins.shape[2]), jnp.bfloat16),
            jax.ShapeDtypeStruct((seed.shape[0], columns), jnp.bfloat16),
        ],
        in_specs=[VMEM] * 2,
        out_specs=[VMEM] * 2,
        compiler_params=limit(4),
        cost_estimate=pl.CostEstimate(flops=1 << 32, bytes_accessed=1 << 24, transcendentals=0),
        name="hold",
    )(spins, seed)


def prepare(hop_matrix, pieces):
    sites = hop_matrix.shape[0]
    width = sum(piece.shape[1] for piece in pieces)
    square = jax.ShapeDtypeStruct((sites, sites), jnp.bfloat16)
    return pl.pallas_call(
        prepare_kernel,
        out_shape=[square] * 3 + [jax.ShapeDtypeStruct((width, sites), jnp.bfloat16)],
        in_specs=[VMEM] * (1 + len(pieces)),
        out_specs=[VMEM] * 4,
        compiler_params=limit(8),
        cost_estimate=pl.CostEstimate(flops=1 << 28, bytes_accessed=1 << 22, transcendentals=0),
        name="prepare",
    )(hop_matrix, *pieces)


def lift(seed_t, high_t, low_t, vertex):
    width, sites = seed_t.shape
    return pl.pallas_call(
        lift_kernel,
        out_shape=jax.ShapeDtypeStruct((width, sites), jnp.float32),
        in_specs=[VMEM] * 4,
        out_specs=VMEM,
        compiler_params=limit(16),
        cost_estimate=work(width, sites, 2),
        name="lift",
    )(seed_t, high_t, low_t, vertex)


def join(held, came):
    shape = (held.shape[0] + came.shape[0], held.shape[1])
    return pl.pallas_call(
        join_kernel,
        out_shape=jax.ShapeDtypeStruct(shape, held.dtype),
        in_specs=[VMEM] * 2,
        out_specs=VMEM,
        compiler_params=limit(4),
        name="join",
    )(held, came)


def start_own(wraps, image, high_t, low_t, lines, doubled):
    width, sites = image.shape
    return pl.pallas_call(
        functools.partial(early_kernel, lax.axis_size("rowt"), doubled),
        out_shape=[
            jax.ShapeDtypeStruct((1, width, sites), jnp.bfloat16),
            jax.ShapeDtypeStruct((width, sites), jnp.float32),
            jax.ShapeDtypeStruct((wraps, sites), jnp.float32),
            jax.ShapeDtypeStruct((wraps, sites, LANES), jnp.float32),
        ],
        in_specs=[VMEM] * (3 + len(lines)),
        out_specs=[VMEM] * 4,
        compiler_params=limit(16),
        cost_estimate=work(width, sites, 2),
        name="early",
    )(image, high_t, low_t, *lines)


def propagate(first, last, image, high_t, low_t, scale):
    (width, sites), wraps = image.shape, scale.shape[0]
    outs = [jax.ShapeDtypeStruct((last - first, width, sites), jnp.bfloat16)]
    if last < wraps:
        outs.append(jax.ShapeDtypeStruct((width, sites), jnp.float32))
    return pl.pallas_call(
        functools.partial(own_kernel, first),
        out_shape=outs,
        in_specs=[VMEM] * 4,
        out_specs=[VMEM] * len(outs),
        compiler_params=limit(16),
        cost_estimate=work(width, sites, 2 * (last - first)),
    )(image, high_t, low_t, scale)


def work(columns, sites, wraps):
    return pl.CostEstimate(
        flops=wraps * sites * sites * columns // 16, bytes_accessed=1 << 16, transcendentals=0
    )


def chain(arrived, hop, scale, width):
    sites, columns = arrived.shape
    wraps = scale.shape[0]
    shape = jax.ShapeDtypeStruct((wraps, width, columns), jnp.bfloat16)
    return pl.pallas_call(
        chain_kernel,
        out_shape=[shape] * 2,
        in_specs=[VMEM] * 3,
        out_specs=[VMEM] * 2,
        compiler_params=limit(16),
        cost_estimate=work(columns, sites, wraps),
        name="chain",
    )(arrived, hop, scale)


def add_up(offset, met, vertex, turned, total=None):
    _, width, columns = met.shape
    sites = vertex.shape[0]
    extra = [] if total is None else [total]
    return pl.pallas_call(
        functools.partial(add_kernel, offset, len(extra)),
        out_shape=jax.ShapeDtypeStruct((sites, width), jnp.float32),
        in_specs=[VMEM] * (2 + len(extra) + len(turned)),
        out_specs=VMEM,
        compiler_params=limit(16),
        cost_estimate=work(columns, sites, 1),
    )(met, vertex, *extra, *turned)


def fold(hop, scale, width):
    sites = hop.shape[0]
    return pl.pallas_call(
        fold_kernel,
        out_shape=jax.ShapeDtypeStruct((width, sites), jnp.bfloat16),
        in_specs=[VMEM] * 2,
        out_specs=VMEM,
        compiler_params=limit(16),
        cost_estimate=work(width, sites, 1),
        name="fold",
    )(hop, scale)


def finish(offset, ours, theirs, hop, folded, columns, vertex, total, turned):
    sites, width = total.shape
    blocks = 3
    return pl.pallas_call(
        functools.partial(finish_kernel, offset),
        out_shape=jax.ShapeDtypeStruct((sites, width), jnp.bfloat16),
        in_specs=[VMEM] * (7 + len(turned)),
        out_specs=HBM,
        scratch_shapes=[
            pltpu.VMEM((sites, width), jnp.bfloat16),
            pltpu.SemaphoreType.DMA((blocks,)),
        ],
        compiler_params=limit(16),
        cost_estimate=work(2 * ours.shape[1], sites, columns.shape[0]),
        name="finish",
    )(ours, theirs, hop, folded, columns, vertex, total, *turned)


def fetch_lines(lines):
    rows, count = lax.axis_size("rowt"), lines.shape[0]
    sites = lax.axis_size("site")
    if rows == count and rows & (rows - 1) == 0:
        bit = 1
        while bit < rows:
            pairs = [
                (i * sites + core, (i ^ bit) * sites + sites - 1 - core)
                for i in range(rows)
                for core in range(sites)
            ]
            came = lax.ppermute(lines, ("rowt", "site"), pairs)
            bit *= 2
            if bit < rows:
                lines = join(lines, came)
        return [lines, came], True
    found = []
    for step in range(count):
        line, shift = lines[step : step + 1], (step + 1) % rows
        if shift:
            line = lax.ppermute(line, "rowt", [((i + shift) % rows, i) for i in range(rows)])
        found.append(line)
    return found, False


def per_device(seed_green, field_spins, hop_matrix, vertex):
    cols, sites = lax.axis_size("colt"), lax.axis_size("site")
    wraps, width = field_spins.shape[0], seed_green.shape[-1]
    edge = width - LANES
    across = [
        (i * sites + core, (i + cols // 2) % cols * sites + sites - 1 - core)
        for i in range(cols)
        for core in range(sites)
    ]
    swap = [(i, sites - 1 - i) for i in range(sites)]

    seed = seed_green[0, 0]
    pieces = [cut(seed, edge)]
    first = lax.ppermute(pieces[0], ("colt", "site"), across)
    lines, piece = hold(field_spins, seed, width - edge)
    pieces.append(piece)
    second = lax.ppermute(piece, ("colt", "site"), across)
    found, doubled = fetch_lines(lines)
    hop, high_t, low_t, seed_t = prepare(hop_matrix, pieces)
    image = lift(seed_t, high_t, low_t, vertex)
    early, image, scale, columns = start_own(wraps, image, high_t, low_t, found, doubled)
    own = (high_t, low_t, scale)
    middle, level = propagate(1, 2, image, *own)
    keep, send = chain(first, hop, columns, width)
    came = lax.ppermute(send, "site", swap)
    (rest,) = propagate(2, wraps, level, *own)
    other = lax.ppermute(second, "site", swap)
    turned = [early, middle, rest]
    total = add_up(0, keep, vertex, turned)
    folded = fold(hop, scale, width)
    total = add_up(0, came, vertex, turned, total)
    result = finish(edge, second, other, hop, folded, columns, vertex, total, turned)
    return result[None, None]


def solution(mesh):
    return jax.shard_map(
        per_device,
        mesh=mesh,
        in_specs=(
            P(("groups", "rowt"), "colt", None, "site"),
            P(None, ("groups", "rowt"), None),
            P(),
            P(),
        ),
        out_specs=P(("groups", "rowt"), "colt", None, "site"),
        check_vma=False,
    )
```

profile of v0, /device:TPU:0, one launch (start us, length us, event | category | flops | bytes accessed | tf_op | source)
XLA Modules:
  0.0 28.9 jit_solution(7033238297675646443)
XLA Ops:
  0.0 0.0 copy-start.2
  0.0 0.0 copy-start.3
  0.0 1.1 %cut.1.refs_0_ = bf16[768,256]{1,0:T(8,128)(2,1)S(1)} custom-call(bf16[768,384]{1,0:T(8,128)(2,1)} %bitcast.2), custom_call_target="tpu_custom_call" | custom-call | flops 1073741824 | bytes 1048576 | tf_op jit(solution)/shard_map/cut/pallas_call | solution.py:273
  1.1 2.5 %collective-permute-start.4 = (bf16[768,256]{1,0:T(8,128)(2,1)S(1)}, bf16[768,256]{1,0:T(8,128)(2,1)S(1)}, u32[]{:S(2)}, u32[]{:S(2)}) collective-permute-start(bf16[768,256]{1,0:T(8,128)(2,1)S(1)} %cut.1.refs_0_), channel_id=1, source_target_pairs={{0,3},{1,2},{2,1},{3,0},{4,7},{5,6},{6,5},{7,4},{8,11},{9,10},{10,... | collective-permute-start | bytes 1179656 | tf_op jit(solution)/shard_map/ppermute | solution.py:477
  3.6 0.0 copy-done.2
  3.6 0.0 copy-done.3
  3.6 0.0 copy-start.1
  3.6 1.9 %collective-permute-start.2 = (bf16[4,768]{1,0:T(4,128)(2,1)S(1)}, bf16[4,768]{1,0:T(4,128)(2,1)S(1)}, u32[]{:S(2)}, u32[]{:S(2)}) collective-permute-start(bf16[4,768]{1,0:T(4,128)(2,1)S(1)} %get-tuple-element.24.held_ref), channel_id=1, source_target_pairs={{0,5},{1,4},{4,1},{5,0},{8,13},{9,12},{12,9},{13,8},{2,7},{3,6},{6... | collective-permute-start | bytes 18440 | tf_op jit(solution)/shard_map/ppermute | solution.py:450
  5.6 1.3 %collective-permute-done.2.came_ref = bf16[4,768]{1,0:T(4,128)(2,1)S(1)} collective-permute-done((bf16[4,768]{1,0:T(4,128)(2,1)S(1)}, bf16[4,768]{1,0:T(4,128)(2,1)S(1)}, u32[]{:S(2)}, u32[]{:S(2)}) %collective-permute-start.2) | collective-permute-done | bytes 6176 | tf_op jit(solution)/shard_map/ppermute | solution.py:450
  6.9 3.1 %collective-permute-start.3 = (bf16[8,768]{1,0:T(8,128)(2,1)S(1)}, bf16[8,768]{1,0:T(8,128)(2,1)S(1)}, u32[]{:S(2)}, u32[]{:S(2)}) collective-permute-start(bf16[8,768]{1,0:T(8,128)(2,1)S(1)} %join.1.refs_0_), channel_id=1, source_target_pairs={{0,9},{1,8},{4,13},{5,12},{8,1},{9,0},{12,5},{13,4},{2,11},{3,10},... | collective-permute-start | bytes 36872 | tf_op jit(solution)/shard_map/ppermute | solution.py:450
  10.0 0.0 copy-done.1
  10.0 0.0 copy-start
  10.0 1.0 %prepare.1 = (bf16[768,768]{1,0:T(8,128)(2,1)S(1)}, bf16[768,768]{1,0:T(8,128)(2,1)S(1)}, bf16[768,768]{1,0:T(8,128)(2,1)S(1)}, bf16[384,768]{1,0:T(8,128)(2,1)S(1)}) custom-call(f32[768,768]{1,0:T(8,128)S(1)} %copy-done.1, bf16[768,256]{1,0:T(8,128)(2,1)S(1)} %cut.1.refs_0_, bf16[768,128]{1,0:T(8,128)(2,1)S(1)} %get-tuple-element.19.refs_1_), custom_call_target="tpu_custom_call" | custom-call | flops 268435456 | bytes 4194304 | tf_op jit(solution)/shard_map/prepare/pallas_call | solution.py:304
  11.1 0.2 copy-done
  11.3 1.1 %lift.1.image_ref = f32[384,768]{1,0:T(8,128)S(1)} custom-call(bf16[384,768]{1,0:T(8,128)(2,1)S(1)} %get-tuple-element.21.seed_t, bf16[768,768]{1,0:T(8,128)(2,1)S(1)} %get-tuple-element.22.high_t, bf16[768,768]{1,0:T(8,128)(2,1)S(1)} %get-tuple-element.23.low_t, bf16[768,768]{1,0:T(8,128)(2,1)S(1)} %copy-done), custom_call_target="tpu_custom_call" | custom-call | flops 28311552 | bytes 65536 | tf_op jit(solution)/shard_map/lift/pallas_call | solution.py:317
  12.4 0.0 collective-permute-done.3.refs_1_
  12.4 1.2 %early.1 = (bf16[1,384,768]{2,1,0:T(8,128)(2,1)S(1)}, f32[384,768]{1,0:T(8,128)S(1)}, f32[4,768]{1,0:T(4,128)S(1)}, f32[4,768,128]{2,1,0:T(8,128)S(1)}) custom-call(f32[384,768]{1,0:T(8,128)S(1)} %lift.1.image_ref, bf16[768,768]{1,0:T(8,128)(2,1)S(1)} %get-tuple-element.22.high_t, bf16[768,768]{1,0:T(8,128)(2,1)S(1)} %get-tuple-element.23.low_t, ...), custom_call_target="tpu_custom_call" | custom-call | flops 28311552 | bytes 65536 | tf_op jit(solution)/shard_map/early/pallas_call | solution.py:342
  13.6 0.0 collective-permute-done.4.arrived
  13.6 1.7 %chain.1 = (bf16[4,384,256]{2,1,0:T(8,128)(2,1)S(1)}, bf16[4,384,256]{2,1,0:T(8,128)(2,1)S(1)}) custom-call(bf16[768,256]{1,0:T(8,128)(2,1)S(1)} %collective-permute-done.4.arrived, bf16[768,768]{1,0:T(8,128)(2,1)S(1)} %get-tuple-element.20.hop_ref.refs_2_, f32[4,768,128]{2,1,0:T(8,128)S(1)} %get-tuple-element.26.scale_ref.refs_4_), custom_call_target="tpu_custom_call" | custom-call | flops 37748736 | bytes 65536 | tf_op jit(solution)/shard_map/chain/pallas_call | solution.py:383
  15.3 0.1 collective-permute-start.5
  15.4 2.0 %collective-permute-start = (bf16[768,128]{1,0:T(8,128)(2,1)S(1)}, bf16[768,128]{1,0:T(8,128)(2,1)S(1)}, u32[]{:S(2)}, u32[]{:S(2)}) collective-permute-start(bf16[768,128]{1,0:T(8,128)(2,1)S(1)} %get-tuple-element.19.refs_1_), channel_id=1, source_target_pairs={{0,3},{1,2},{2,1},{3,0},{4,7},{5,6},{6,5},{7,4},{8,11},{9,10},{10,... | collective-permute-start | bytes 589832 | tf_op jit(solution)/shard_map/ppermute | solution.py:480
  17.4 5.1 %collective-permute-done.refs_0_ = bf16[768,128]{1,0:T(8,128)(2,1)S(1)} collective-permute-done((bf16[768,128]{1,0:T(8,128)(2,1)S(1)}, bf16[768,128]{1,0:T(8,128)(2,1)S(1)}, u32[]{:S(2)}, u32[]{:S(2)}) %collective-permute-start) | collective-permute-done | bytes 196640 | tf_op jit(solution)/shard_map/ppermute | solution.py:480
  22.5 0.2 collective-permute-start.1
  22.7 0.6 %fold.1.refs_3_ = bf16[384,768]{1,0:T(8,128)(2,1)S(1)} custom-call(bf16[768,768]{1,0:T(8,128)(2,1)S(1)} %get-tuple-element.20.hop_ref.refs_2_, f32[4,768]{1,0:T(4,128)S(1)} %get-tuple-element.25.scale_ref), custom_call_target="tpu_custom_call" | custom-call | flops 14155776 | bytes 65536 | tf_op jit(solution)/shard_map/fold/pallas_call | solution.py:410
  23.3 1.1 %shard_map.46 = (bf16[1,384,768]{2,1,0:T(8,128)(2,1)S(1)}, f32[384,768]{1,0:T(8,128)S(1)}) custom-call(f32[384,768]{1,0:T(8,128)S(1)} %get-tuple-element.30.image_ref, bf16[768,768]{1,0:T(8,128)(2,1)S(1)} %get-tuple-element.22.high_t, bf16[768,768]{1,0:T(8,128)(2,1)S(1)} %get-tuple-element.23.low_t, f32[4,768]{1,0:T(4,128)S(1)} %get-tuple-element.25.scale_ref), custom_call_target="tpu_custom_call" | custom-call | flops 28311552 | bytes 65536 | tf_op jit(solution)/shard_map/pallas_call | solution.py:363
  24.4 0.7 %shard_map.47.refs_2_.refs_3_.refs_9_ = bf16[2,384,768]{2,1,0:T(8,128)(2,1)S(1)} custom-call(f32[384,768]{1,0:T(8,128)S(1)} %get-tuple-element.32.image_ref, bf16[768,768]{1,0:T(8,128)(2,1)S(1)} %get-tuple-element.22.high_t, bf16[768,768]{1,0:T(8,128)(2,1)S(1)} %get-tuple-element.23.low_t, f32[4,768]{1,0:T(4,128)S(1)} %get-tuple-element.25.scale_ref), custom_call_target="tpu_custom_call" | custom-call | flops 56623104 | bytes 65536 | tf_op jit(solution)/shard_map/pallas_call | solution.py:363
  25.1 0.7 %shard_map.48.refs_0_ = f32[768,384]{1,0:T(8,128)S(1)} custom-call(bf16[4,384,256]{2,1,0:T(8,128)(2,1)S(1)} %get-tuple-element.28.met_ref, bf16[768,768]{1,0:T(8,128)(2,1)S(1)} %copy-done, bf16[1,384,768]{2,1,0:T(8,128)(2,1)S(1)} %get-tuple-element.29.refs_0_.refs_1_.refs_7_, bf16[1,384,768]{2,1,0:T(8,128)(2,1)S(1)} %get-tuple-element.31.refs_1_.refs_2_.refs_8_, ...), custom_call_target="tpu_custom_call" | custom-call | flops 9437184 | bytes 65536 | tf_op jit(solution)/shard_map/pallas_call | solution.py:398
  25.8 0.0 collective-permute-done.5.met_ref
  25.8 0.7 %shard_map.49.refs_6_ = f32[768,384]{1,0:T(8,128)S(1)} custom-call(bf16[4,384,256]{2,1,0:T(8,128)(2,1)S(1)} %collective-permute-done.5.met_ref, bf16[768,768]{1,0:T(8,128)(2,1)S(1)} %copy-done, f32[768,384]{1,0:T(8,128)S(1)} %shard_map.48.refs_0_, bf16[1,384,768]{2,1,0:T(8,128)(2,1)S(1)} %get-tuple-element.29.refs_0_.refs_1_.refs_7_, ...), custom_call_target="tpu_custom_call" | custom-call | flops 9437184 | bytes 65536 | tf_op jit(solution)/shard_map/pallas_call | solution.py:398
  26.5 0.0 collective-permute-done.1.refs_1_
  26.6 2.4 %finish.1 = bf16[768,384]{1,0:T(8,128)(2,1)} custom-call(bf16[768,128]{1,0:T(8,128)(2,1)S(1)} %collective-permute-done.refs_0_, bf16[768,128]{1,0:T(8,128)(2,1)S(1)} %collective-permute-done.1.refs_1_, bf16[768,768]{1,0:T(8,128)(2,1)S(1)} %get-tuple-element.20.hop_ref.refs_2_, bf16[384,768]{1,0:T(8,128)(2,1)S(1)} %fold.1.refs_3_, ...), custom_call_target="tpu_custom_call" | custom-call | flops 37748736 | bytes 65536 | tf_op jit(solution)/shard_map/finish/pallas_call | solution.py:424
  (2 shorter events, 0.1 us)
Async XLA Ops:
  0.0 3.6 %copy-start.2 = (bf16[1,1,768,384]{3,2,1,0:T(8,128)(2,1)S(1)}, bf16[1,1,768,384]{3,2,1,0:T(8,128)(2,1)}, u32[]{:S(2)}) copy-start(bf16[1,1,768,384]{3,2,1,0:T(8,128)(2,1)} %param.4) | copy-start | bytes 1769476
  0.0 3.6 %copy-start.3 = (s32[4,1,768]{2,1,0:T(1,128)S(1)}, s32[4,1,768]{2,1,0:T(1,128)}, u32[]{:S(2)}) copy-start(s32[4,1,768]{2,1,0:T(1,128)} %spins_ref.1) | copy-start | bytes 36868
  1.1 12.5 %collective-permute-start.4 = (bf16[768,256]{1,0:T(8,128)(2,1)S(1)}, bf16[768,256]{1,0:T(8,128)(2,1)S(1)}, u32[]{:S(2)}, u32[]{:S(2)}) collective-permute-start(bf16[768,256]{1,0:T(8,128)(2,1)S(1)} %cut.1.refs_0_), channel_id=1, source_target_pairs={{0,3},{1,2},{2,1},{3,0},{4,7},{5,6},{6,5},{7,4},{8,11},{9,10},{10,... | collective-permute-start | bytes 1179656 | tf_op jit(solution)/shard_map/ppermute | solution.py:477
  3.6 6.4 %copy-start.1 = (f32[768,768]{1,0:T(8,128)S(1)}, f32[768,768]{1,0:T(8,128)}, u32[]{:S(2)}) copy-start(f32[768,768]{1,0:T(8,128)} %hop_ref.1) | copy-start | bytes 7077892
  3.6 3.3 %collective-permute-start.2 = (bf16[4,768]{1,0:T(4,128)(2,1)S(1)}, bf16[4,768]{1,0:T(4,128)(2,1)S(1)}, u32[]{:S(2)}, u32[]{:S(2)}) collective-permute-start(bf16[4,768]{1,0:T(4,128)(2,1)S(1)} %get-tuple-element.24.held_ref), channel_id=1, source_target_pairs={{0,5},{1,4},{4,1},{5,0},{8,13},{9,12},{12,9},{13,8},{2,7},{3,6},{6... | collective-permute-start | bytes 18440 | tf_op jit(solution)/shard_map/ppermute | solution.py:450
  6.9 5.5 %collective-permute-start.3 = (bf16[8,768]{1,0:T(8,128)(2,1)S(1)}, bf16[8,768]{1,0:T(8,128)(2,1)S(1)}, u32[]{:S(2)}, u32[]{:S(2)}) collective-permute-start(bf16[8,768]{1,0:T(8,128)(2,1)S(1)} %join.1.refs_0_), channel_id=1, source_target_pairs={{0,9},{1,8},{4,13},{5,12},{8,1},{9,0},{12,5},{13,4},{2,11},{3,10},... | collective-permute-start | bytes 36872 | tf_op jit(solution)/shard_map/ppermute | solution.py:450
  10.0 1.3 %copy-start = (bf16[768,768]{1,0:T(8,128)(2,1)S(1)}, bf16[768,768]{1,0:T(8,128)(2,1)}, u32[]{:S(2)}) copy-start(bf16[768,768]{1,0:T(8,128)(2,1)} %refs_5_.1) | copy-start | bytes 3538948
  15.3 10.6 %collective-permute-start.5 = (bf16[4,384,256]{2,1,0:T(8,128)(2,1)S(1)}, bf16[4,384,256]{2,1,0:T(8,128)(2,1)S(1)}, u32[]{:S(2)}, u32[]{:S(2)}) collective-permute-start(bf16[4,384,256]{2,1,0:T(8,128)(2,1)S(1)} %get-tuple-element.27), channel_id=1, source_target_pairs={{0,1},{1,0},{2,3},{3,2},{4,5},{5,4},{6,7},{7,6},{8,9},{9,8},{10,11... | collective-permute-start | bytes 2359304 | tf_op jit(solution)/shard_map/ppermute | solution.py:488
  15.4 7.1 %collective-permute-start = (bf16[768,128]{1,0:T(8,128)(2,1)S(1)}, bf16[768,128]{1,0:T(8,128)(2,1)S(1)}, u32[]{:S(2)}, u32[]{:S(2)}) collective-permute-start(bf16[768,128]{1,0:T(8,128)(2,1)S(1)} %get-tuple-element.19.refs_1_), channel_id=1, source_target_pairs={{0,3},{1,2},{2,1},{3,0},{4,7},{5,6},{6,5},{7,4},{8,11},{9,10},{10,... | collective-permute-start | bytes 589832 | tf_op jit(solution)/shard_map/ppermute | solution.py:480
  22.5 4.1 %collective-permute-start.1 = (bf16[768,128]{1,0:T(8,128)(2,1)S(1)}, bf16[768,128]{1,0:T(8,128)(2,1)S(1)}, u32[]{:S(2)}, u32[]{:S(2)}) collective-permute-start(bf16[768,128]{1,0:T(8,128)(2,1)S(1)} %collective-permute-done.refs_0_), channel_id=1, source_target_pairs={{0,1},{1,0},{2,3},{3,2},{4,5},{5,4},{6,7},{7,6},{8,9},{9,8},{10,11... | collective-permute-start | bytes 589832 | tf_op jit(solution)/shard_map/ppermute | solution.py:490
where the time goes:
time: 29.1 us; the launch traced here: 28.9 us
  Pallas kernels  12.3 us (42%)
  starting transfers between devices  9.79 us (34%)
  waiting for transfers between devices  6.44 us (22%)
    ppermute x1, waiting for transfers between devices, per_device(): second = lax.ppermute(piece, ('colt', 'site'), across)  5.08 us
    ppermute x2, starting transfers between devices, fetch_lines(): came = lax.ppermute(lines, ('rowt', 'site'), pairs)  5 us
    ppermute x1, starting transfers between devices, per_device(): first = lax.ppermute(pieces[0], ('colt', 'site'), across)  2.47 us
    pallas_call x1, Pallas kernels, finish(): pl.pallas_call(functools.partial(finish_kernel, offset), out_shape=jax.Sh...  2.38 us
    ppermute x1, starting transfers between devices, per_device(): second = lax.ppermute(piece, ('colt', 'site'), across)  2.04 us
    pallas_call x2, Pallas kernels, propagate(): pl.pallas_call(functools.partial(own_kernel, first), out_shape=outs, in_s...  1.8 us
    pallas_call x1, Pallas kernels, chain(): pl.pallas_call(chain_kernel, out_shape=[shape] * 2, in_specs=[VMEM] * 3,...  1.67 us
    pallas_call x2, Pallas kernels, add_up(): pl.pallas_call(functools.partial(add_kernel, offset, len(extra)), out_sha...  1.38 us
  transfers between devices with their start and end apart: 6, of which 2 were waited for; matrix products, arithmetic and copies ran while one was open for 0% of the time, Pallas kernels for 25%

commit v1 on v0

--- a/solution.py
+++ b/solution.py
@@ -122,10 +122,13 @@
             spins = lines[step : step + 1]
         sign = jnp.where(target == 0, -1.0, 1.0)
         scales.append(sign * jnp.exp(coupling * (2.0 * spins - 1.0)))
-    turned = scales[0] * image_ref[...]
-    narrow = turned.astype(jnp.bfloat16)
-    turned_out[0] = narrow
-    image_out[...] = keep_share * turned + hop_turned(narrow, high_t, low_t)
+    image = image_ref[...]
+    for step in range(turned_out.shape[0]):
+        turned = scales[step] * image
+        narrow = turned.astype(jnp.bfloat16)
+        turned_out[step] = narrow
+        image = keep_share * turned + hop_turned(narrow, high_t, low_t)
+    image_out[...] = image
     scale = jnp.concatenate(scales, axis=0)
     scale_out[...] = scale
     columns = scale.T
@@ -342,7 +345,7 @@
     return pl.pallas_call(
         functools.partial(early_kernel, lax.axis_size("rowt"), doubled),
         out_shape=[
-            jax.ShapeDtypeStruct((1, width, sites), jnp.bfloat16),
+            jax.ShapeDtypeStruct((wraps // 2, width, sites), jnp.bfloat16),
             jax.ShapeDtypeStruct((width, sites), jnp.float32),
             jax.ShapeDtypeStruct((wraps, sites), jnp.float32),
             jax.ShapeDtypeStruct((wraps, sites, LANES), jnp.float32),
@@ -483,12 +486,11 @@
     image = lift(seed_t, high_t, low_t, vertex)
     early, image, scale, columns = start_own(wraps, image, high_t, low_t, found, doubled)
     own = (high_t, low_t, scale)
-    middle, level = propagate(1, 2, image, *own)
     keep, send = chain(first, hop, columns, width)
     came = lax.ppermute(send, "site", swap)
-    (rest,) = propagate(2, wraps, level, *own)
+    (rest,) = propagate(wraps // 2, wraps, image, *own)
     other = lax.ppermute(second, "site", swap)
-    turned = [early, middle, rest]
+    turned = [early, rest]
     total = add_up(0, keep, vertex, turned)
     folded = fold(hop, scale, width)
     total = add_up(0, came, vertex, turned, total)

time: 29.1 us -> 29 us (level)
  starting transfers between devices: 9.79 us -> 8.73 us
  waiting for transfers between devices: 6.44 us -> 7.26 us
    pallas_call x1, Pallas kernels: 1.2 us -> 2.51 us  [start_own(): pl.pallas_call(functools.partial(early_kernel, lax.axis_size('rowt'), dou...]
    ppermute x1, starting transfers between devices: 2.04 us -> 0.75 us  [per_device(): second = lax.ppermute(piece, ('colt', 'site'), across)]
    pallas_call x2 -> x1, Pallas kernels: 1.8 us -> 0.66 us  [propagate(): pl.pallas_call(functools.partial(own_kernel, first), out_shape=outs, in_s...]
    ppermute x1, waiting for transfers between devices: 5.08 us -> 5.9 us  [per_device(): second = lax.ppermute(piece, ('colt', 'site'), across)]
  transfers between devices with their start and end apart: 6 -> 6, of which waited for: 2 -> 2; matrix products, arithmetic and copies ran while one was open for 0% -> 0% of each run, Pallas kernels for 25% -> 26%
where the time goes in v1:
time: 29 us; the launch traced here: 28.8 us
  Pallas kernels  12.5 us (43%)
  starting transfers between devices  8.73 us (30%)
  waiting for transfers between devices  7.26 us (25%)
    ppermute x1, waiting for transfers between devices, per_device(): second = lax.ppermute(piece, ('colt', 'site'), across)  5.9 us
    ppermute x2, starting transfers between devices, fetch_lines(): came = lax.ppermute(lines, ('rowt', 'site'), pairs)  5 us
    pallas_call x1, Pallas kernels, start_own(): pl.pallas_call(functools.partial(early_kernel, lax.axis_size('rowt'), dou...  2.51 us
    ppermute x1, starting transfers between devices, per_device(): first = lax.ppermute(pieces[0], ('colt', 'site'), across)  2.47 us
    pallas_call x1, Pallas kernels, finish(): pl.pallas_call(functools.partial(finish_kernel, offset), out_shape=jax.Sh...  2.37 us
    pallas_call x1, Pallas kernels, chain(): pl.pallas_call(chain_kernel, out_shape=[shape] * 2, in_specs=[VMEM] * 3,...  1.67 us
    pallas_call x2, Pallas kernels, add_up(): pl.pallas_call(functools.partial(add_kernel, offset, len(extra)), out_sha...  1.38 us
    ppermute x2, waiting for transfers between devices, fetch_lines(): came = lax.ppermute(lines, ('rowt', 'site'), pairs)  1.35 us
  transfers between devices with their start and end apart: 6, of which 2 were waited for; matrix products, arithmetic and copies ran while one was open for 0% of the time, Pallas kernels for 26%

profile of v1, /device:TPU:0, one launch (start us, length us, event | category | flops | bytes accessed | tf_op | source)
XLA Modules:
  0.0 28.8 jit_solution(13143823464500270982)
XLA Ops:
  0.0 0.0 copy-start.2
  0.0 0.0 copy-start.3
  0.0 1.1 %cut.1.refs_0_ = bf16[768,256]{1,0:T(8,128)(2,1)S(1)} custom-call(bf16[768,384]{1,0:T(8,128)(2,1)} %bitcast.2), custom_call_target="tpu_custom_call" | custom-call | flops 1073741824 | bytes 1048576 | tf_op jit(solution)/shard_map/cut/pallas_call | solution.py:276
  1.1 2.5 %collective-permute-start.4 = (bf16[768,256]{1,0:T(8,128)(2,1)S(1)}, bf16[768,256]{1,0:T(8,128)(2,1)S(1)}, u32[]{:S(2)}, u32[]{:S(2)}) collective-permute-start(bf16[768,256]{1,0:T(8,128)(2,1)S(1)} %cut.1.refs_0_), channel_id=1, source_target_pairs={{0,3},{1,2},{2,1},{3,0},{4,7},{5,6},{6,5},{7,4},{8,11},{9,10},{10,... | collective-permute-start | bytes 1179656 | tf_op jit(solution)/shard_map/ppermute | solution.py:480
  3.6 0.0 copy-done.2
  3.6 0.0 copy-done.3
  3.6 0.0 copy-start.1
  3.6 1.9 %collective-permute-start.2 = (bf16[4,768]{1,0:T(4,128)(2,1)S(1)}, bf16[4,768]{1,0:T(4,128)(2,1)S(1)}, u32[]{:S(2)}, u32[]{:S(2)}) collective-permute-start(bf16[4,768]{1,0:T(4,128)(2,1)S(1)} %get-tuple-element.22.held_ref), channel_id=1, source_target_pairs={{0,5},{1,4},{4,1},{5,0},{8,13},{9,12},{12,9},{13,8},{2,7},{3,6},{6... | collective-permute-start | bytes 18440 | tf_op jit(solution)/shard_map/ppermute | solution.py:453
  5.6 1.3 %collective-permute-done.2.came_ref = bf16[4,768]{1,0:T(4,128)(2,1)S(1)} collective-permute-done((bf16[4,768]{1,0:T(4,128)(2,1)S(1)}, bf16[4,768]{1,0:T(4,128)(2,1)S(1)}, u32[]{:S(2)}, u32[]{:S(2)}) %collective-permute-start.2) | collective-permute-done | bytes 6176 | tf_op jit(solution)/shard_map/ppermute | solution.py:453
  6.9 3.1 %collective-permute-start.3 = (bf16[8,768]{1,0:T(8,128)(2,1)S(1)}, bf16[8,768]{1,0:T(8,128)(2,1)S(1)}, u32[]{:S(2)}, u32[]{:S(2)}) collective-permute-start(bf16[8,768]{1,0:T(8,128)(2,1)S(1)} %join.1.refs_0_), channel_id=1, source_target_pairs={{0,9},{1,8},{4,13},{5,12},{8,1},{9,0},{12,5},{13,4},{2,11},{3,10},... | collective-permute-start | bytes 36872 | tf_op jit(solution)/shard_map/ppermute | solution.py:453
  10.0 0.0 copy-done.1
  10.0 0.0 copy-start
  10.0 1.0 %prepare.1 = (bf16[768,768]{1,0:T(8,128)(2,1)S(1)}, bf16[768,768]{1,0:T(8,128)(2,1)S(1)}, bf16[768,768]{1,0:T(8,128)(2,1)S(1)}, bf16[384,768]{1,0:T(8,128)(2,1)S(1)}) custom-call(f32[768,768]{1,0:T(8,128)S(1)} %copy-done.1, bf16[768,256]{1,0:T(8,128)(2,1)S(1)} %cut.1.refs_0_, bf16[768,128]{1,0:T(8,128)(2,1)S(1)} %get-tuple-element.17.refs_1_), custom_call_target="tpu_custom_call" | custom-call | flops 268435456 | bytes 4194304 | tf_op jit(solution)/shard_map/prepare/pallas_call | solution.py:307
  11.1 0.2 copy-done
  11.3 1.1 %lift.1.image_ref = f32[384,768]{1,0:T(8,128)S(1)} custom-call(bf16[384,768]{1,0:T(8,128)(2,1)S(1)} %get-tuple-element.19.seed_t, bf16[768,768]{1,0:T(8,128)(2,1)S(1)} %get-tuple-element.20.high_t, bf16[768,768]{1,0:T(8,128)(2,1)S(1)} %get-tuple-element.21.low_t, bf16[768,768]{1,0:T(8,128)(2,1)S(1)} %copy-done), custom_call_target="tpu_custom_call" | custom-call | flops 28311552 | bytes 65536 | tf_op jit(solution)/shard_map/lift/pallas_call | solution.py:320
  12.4 0.0 collective-permute-done.3.refs_1_
  12.4 2.5 %early.1 = (bf16[2,384,768]{2,1,0:T(8,128)(2,1)S(1)}, f32[384,768]{1,0:T(8,128)S(1)}, f32[4,768]{1,0:T(4,128)S(1)}, f32[4,768,128]{2,1,0:T(8,128)S(1)}) custom-call(f32[384,768]{1,0:T(8,128)S(1)} %lift.1.image_ref, bf16[768,768]{1,0:T(8,128)(2,1)S(1)} %get-tuple-element.20.high_t, bf16[768,768]{1,0:T(8,128)(2,1)S(1)} %get-tuple-element.21.low_t, ...), custom_call_target="tpu_custom_call" | custom-call | flops 28311552 | bytes 65536 | tf_op jit(solution)/shard_map/early/pallas_call | solution.py:345
  14.9 0.0 collective-permute-done.4.arrived
  14.9 1.7 %chain.1 = (bf16[4,384,256]{2,1,0:T(8,128)(2,1)S(1)}, bf16[4,384,256]{2,1,0:T(8,128)(2,1)S(1)}) custom-call(bf16[768,256]{1,0:T(8,128)(2,1)S(1)} %collective-permute-done.4.arrived, bf16[768,768]{1,0:T(8,128)(2,1)S(1)} %get-tuple-element.18.hop_ref.refs_2_, f32[4,768,128]{2,1,0:T(8,128)S(1)} %get-tuple-element.24.scale_ref.refs_4_), custom_call_target="tpu_custom_call" | custom-call | flops 37748736 | bytes 65536 | tf_op jit(solution)/shard_map/chain/pallas_call | solution.py:386
  16.6 0.1 collective-permute-start.5
  16.7 0.8 %collective-permute-start = (bf16[768,128]{1,0:T(8,128)(2,1)S(1)}, bf16[768,128]{1,0:T(8,128)(2,1)S(1)}, u32[]{:S(2)}, u32[]{:S(2)}) collective-permute-start(bf16[768,128]{1,0:T(8,128)(2,1)S(1)} %get-tuple-element.17.refs_1_), channel_id=1, source_target_pairs={{0,3},{1,2},{2,1},{3,0},{4,7},{5,6},{6,5},{7,4},{8,11},{9,10},{10,... | collective-permute-start | bytes 589832 | tf_op jit(solution)/shard_map/ppermute | solution.py:483
  17.4 5.9 %collective-permute-done.refs_0_ = bf16[768,128]{1,0:T(8,128)(2,1)S(1)} collective-permute-done((bf16[768,128]{1,0:T(8,128)(2,1)S(1)}, bf16[768,128]{1,0:T(8,128)(2,1)S(1)}, u32[]{:S(2)}, u32[]{:S(2)}) %collective-permute-start) | collective-permute-done | bytes 196640 | tf_op jit(solution)/shard_map/ppermute | solution.py:483
  23.3 0.4 %collective-permute-start.1 = (bf16[768,128]{1,0:T(8,128)(2,1)S(1)}, bf16[768,128]{1,0:T(8,128)(2,1)S(1)}, u32[]{:S(2)}, u32[]{:S(2)}) collective-permute-start(bf16[768,128]{1,0:T(8,128)(2,1)S(1)} %collective-permute-done.refs_0_), channel_id=1, source_target_pairs={{0,1},{1,0},{2,3},{3,2},{4,5},{5,4},{6,7},{7,6},{8,9},{9,8},{10,11... | collective-permute-start | bytes 589832 | tf_op jit(solution)/shard_map/ppermute | solution.py:492
  23.7 0.6 %fold.1.refs_3_ = bf16[384,768]{1,0:T(8,128)(2,1)S(1)} custom-call(bf16[768,768]{1,0:T(8,128)(2,1)S(1)} %get-tuple-element.18.hop_ref.refs_2_, f32[4,768]{1,0:T(4,128)S(1)} %get-tuple-element.23.scale_ref), custom_call_target="tpu_custom_call" | custom-call | flops 14155776 | bytes 65536 | tf_op jit(solution)/shard_map/fold/pallas_call | solution.py:413
  24.4 0.7 %shard_map.46.refs_1_.refs_2_.refs_8_ = bf16[2,384,768]{2,1,0:T(8,128)(2,1)S(1)} custom-call(f32[384,768]{1,0:T(8,128)S(1)} %get-tuple-element.28.image_ref, bf16[768,768]{1,0:T(8,128)(2,1)S(1)} %get-tuple-element.20.high_t, bf16[768,768]{1,0:T(8,128)(2,1)S(1)} %get-tuple-element.21.low_t, f32[4,768]{1,0:T(4,128)S(1)} %get-tuple-element.23.scale_ref), custom_call_target="tpu_custom_call" | custom-call | flops 56623104 | bytes 65536 | tf_op jit(solution)/shard_map/pallas_call | solution.py:366
  25.0 0.7 %shard_map.47.refs_0_ = f32[768,384]{1,0:T(8,128)S(1)} custom-call(bf16[4,384,256]{2,1,0:T(8,128)(2,1)S(1)} %get-tuple-element.26.met_ref, bf16[768,768]{1,0:T(8,128)(2,1)S(1)} %copy-done, bf16[2,384,768]{2,1,0:T(8,128)(2,1)S(1)} %get-tuple-element.27.refs_0_.refs_1_.refs_7_, bf16[2,384,768]{2,1,0:T(8,128)(2,1)S(1)} %shard_map.46.refs_1_.refs_2_.refs_8_), custom_call_target="tpu_custom_call" | custom-call | flops 9437184 | bytes 65536 | tf_op jit(solution)/shard_map/pallas_call | solution.py:401
  25.7 0.0 collective-permute-done.5.met_ref
  25.8 0.7 %shard_map.48.refs_6_ = f32[768,384]{1,0:T(8,128)S(1)} custom-call(bf16[4,384,256]{2,1,0:T(8,128)(2,1)S(1)} %collective-permute-done.5.met_ref, bf16[768,768]{1,0:T(8,128)(2,1)S(1)} %copy-done, f32[768,384]{1,0:T(8,128)S(1)} %shard_map.47.refs_0_, bf16[2,384,768]{2,1,0:T(8,128)(2,1)S(1)} %get-tuple-element.27.refs_0_.refs_1_.refs_7_, ...), custom_call_target="tpu_custom_call" | custom-call | flops 9437184 | bytes 65536 | tf_op jit(solution)/shard_map/pallas_call | solution.py:401
  26.4 0.0 collective-permute-done.1.refs_1_
  26.5 2.4 %finish.1 = bf16[768,384]{1,0:T(8,128)(2,1)} custom-call(bf16[768,128]{1,0:T(8,128)(2,1)S(1)} %collective-permute-done.refs_0_, bf16[768,128]{1,0:T(8,128)(2,1)S(1)} %collective-permute-done.1.refs_1_, bf16[768,768]{1,0:T(8,128)(2,1)S(1)} %get-tuple-element.18.hop_ref.refs_2_, bf16[384,768]{1,0:T(8,128)(2,1)S(1)} %fold.1.refs_3_, ...), custom_call_target="tpu_custom_call" | custom-call | flops 37748736 | bytes 65536 | tf_op jit(solution)/shard_map/finish/pallas_call | solution.py:427
  (2 shorter events, 0.1 us)
Async XLA Ops:
  0.0 3.6 %copy-start.2 = (bf16[1,1,768,384]{3,2,1,0:T(8,128)(2,1)S(1)}, bf16[1,1,768,384]{3,2,1,0:T(8,128)(2,1)}, u32[]{:S(2)}) copy-start(bf16[1,1,768,384]{3,2,1,0:T(8,128)(2,1)} %param.4) | copy-start | bytes 1769476
  0.0 3.6 %copy-start.3 = (s32[4,1,768]{2,1,0:T(1,128)S(1)}, s32[4,1,768]{2,1,0:T(1,128)}, u32[]{:S(2)}) copy-start(s32[4,1,768]{2,1,0:T(1,128)} %spins_ref.1) | copy-start | bytes 36868
  1.1 13.8 %collective-permute-start.4 = (bf16[768,256]{1,0:T(8,128)(2,1)S(1)}, bf16[768,256]{1,0:T(8,128)(2,1)S(1)}, u32[]{:S(2)}, u32[]{:S(2)}) collective-permute-start(bf16[768,256]{1,0:T(8,128)(2,1)S(1)} %cut.1.refs_0_), channel_id=1, source_target_pairs={{0,3},{1,2},{2,1},{3,0},{4,7},{5,6},{6,5},{7,4},{8,11},{9,10},{10,... | collective-permute-start | bytes 1179656 | tf_op jit(solution)/shard_map/ppermute | solution.py:480
  3.6 6.4 %copy-start.1 = (f32[768,768]{1,0:T(8,128)S(1)}, f32[768,768]{1,0:T(8,128)}, u32[]{:S(2)}) copy-start(f32[768,768]{1,0:T(8,128)} %hop_ref.1) | copy-start | bytes 7077892
  3.6 3.3 %collective-permute-start.2 = (bf16[4,768]{1,0:T(4,128)(2,1)S(1)}, bf16[4,768]{1,0:T(4,128)(2,1)S(1)}, u32[]{:S(2)}, u32[]{:S(2)}) collective-permute-start(bf16[4,768]{1,0:T(4,128)(2,1)S(1)} %get-tuple-element.22.held_ref), channel_id=1, source_target_pairs={{0,5},{1,4},{4,1},{5,0},{8,13},{9,12},{12,9},{13,8},{2,7},{3,6},{6... | collective-permute-start | bytes 18440 | tf_op jit(solution)/shard_map/ppermute | solution.py:453
  6.9 5.4 %collective-permute-start.3 = (bf16[8,768]{1,0:T(8,128)(2,1)S(1)}, bf16[8,768]{1,0:T(8,128)(2,1)S(1)}, u32[]{:S(2)}, u32[]{:S(2)}) collective-permute-start(bf16[8,768]{1,0:T(8,128)(2,1)S(1)} %join.1.refs_0_), channel_id=1, source_target_pairs={{0,9},{1,8},{4,13},{5,12},{8,1},{9,0},{12,5},{13,4},{2,11},{3,10},... | collective-permute-start | bytes 36872 | tf_op jit(solution)/shard_map/ppermute | solution.py:453
  10.0 1.3 %copy-start = (bf16[768,768]{1,0:T(8,128)(2,1)S(1)}, bf16[768,768]{1,0:T(8,128)(2,1)}, u32[]{:S(2)}) copy-start(bf16[768,768]{1,0:T(8,128)(2,1)} %refs_5_.1) | copy-start | bytes 3538948
  16.6 9.2 %collective-permute-start.5 = (bf16[4,384,256]{2,1,0:T(8,128)(2,1)S(1)}, bf16[4,384,256]{2,1,0:T(8,128)(2,1)S(1)}, u32[]{:S(2)}, u32[]{:S(2)}) collective-permute-start(bf16[4,384,256]{2,1,0:T(8,128)(2,1)S(1)} %get-tuple-element.25), channel_id=1, source_target_pairs={{0,1},{1,0},{2,3},{3,2},{4,5},{5,4},{6,7},{7,6},{8,9},{9,8},{10,11... | collective-permute-start | bytes 2359304 | tf_op jit(solution)/shard_map/ppermute | solution.py:490
  16.7 6.7 %collective-permute-start = (bf16[768,128]{1,0:T(8,128)(2,1)S(1)}, bf16[768,128]{1,0:T(8,128)(2,1)S(1)}, u32[]{:S(2)}, u32[]{:S(2)}) collective-permute-start(bf16[768,128]{1,0:T(8,128)(2,1)S(1)} %get-tuple-element.17.refs_1_), channel_id=1, source_target_pairs={{0,3},{1,2},{2,1},{3,0},{4,7},{5,6},{6,5},{7,4},{8,11},{9,10},{10,... | collective-permute-start | bytes 589832 | tf_op jit(solution)/shard_map/ppermute | solution.py:483
  23.3 3.1 %collective-permute-start.1 = (bf16[768,128]{1,0:T(8,128)(2,1)S(1)}, bf16[768,128]{1,0:T(8,128)(2,1)S(1)}, u32[]{:S(2)}, u32[]{:S(2)}) collective-permute-start(bf16[768,128]{1,0:T(8,128)(2,1)S(1)} %collective-permute-done.refs_0_), channel_id=1, source_target_pairs={{0,1},{1,0},{2,3},{3,2},{4,5},{5,4},{6,7},{7,6},{8,9},{9,8},{10,11... | collective-permute-start | bytes 589832 | tf_op jit(solution)/shard_map/ppermute | solution.py:492
